TPU v7x, 32 devices: a whole 2x2x4 slice. The times are simulated.
32 devices in a mesh: section: 4 (over y, x), dp: 8 (over z, core).
Axes of the slice: x: 2, y: 2, z: 4, core: 2. Of those that a mesh axis runs over, the one named last changes fastest.
Arguments:
- descriptors: bfloat16 [4, 4096, 1024], P(None, 'dp'), may hold values from -6 to 6
- layer_weight: bfloat16 [4, 8, 1024, 1024], P('section', None, 'dp'), may hold values from -0.25 to 0.25
- layer_bias: float32 [4, 8, 1024], P('section'), may hold values from -3 to 3
- readout: float32 [8, 1024], replicated, may hold values from -0.75 to 0.75
- self_energy: float32 [8], replicated, may hold values from -2 to -0.5
- tile_species: int32 [4, 32], P(None, 'dp'), may hold values from 0 to 7
- tile_fill: int32 [4, 32], P(None, 'dp'), may hold values from 1 to 128
Outputs:
- atom_energy: float32 [4, 4096], P('section', 'dp')
- energy: float32 [4], replicated
All inputs are finite; a program needn't handle non-finite values.
Results may differ from a plain program's by a relative error of at most 0.0044.
Values may be sent and summed in bfloat16 or wider, within the bound.
No kernel may reach another device: no remote copies, remote signals or barrier semaphores. Data moves between devices by JAX's collectives and lax.ppermute only.
A program may use at most 128 MiB of HBM per device.

v0:
```python
import jax
import jax.numpy as jnp
from jax import lax
from jax.sharding import PartitionSpec as P


def shifted(block, axis, distance):
    devices = range(lax.axis_size(axis))
    route = [(i - distance, i) for i in devices if i - distance in devices]
    return lax.ppermute(block, axis, route)


def smooth_unit(value):
    return jnp.maximum(value, 0.0) + jnp.minimum(jnp.expm1(jnp.minimum(value, 0.0)), 0.0)


def grouped_product(source, weights, species):
    chosen = jnp.take(weights, species, axis=0)
    return jnp.einsum("tai,tio->tao", source, chosen, preferred_element_type=jnp.float32)


def table_rows(onehot, table):
    return jnp.dot(onehot, table, precision=lax.Precision.HIGHEST)


def shards(descriptors, layer_weight, layer_bias, readout, self_energy, tile_species, tile_fill):
    sections = lax.axis_size("section")
    position = lax.axis_index("section")
    batches, atoms_dev, width = descriptors.shape
    tiles_dev = tile_species.shape[1]
    tile = atoms_dev // tiles_dev
    kinds = readout.shape[0]
    atoms_all = atoms_dev * lax.axis_size("dp")
    total_steps = batches + sections - 1
    bias = layer_bias[0]
    is_last = position == sections - 1
    kind_ids = jnp.arange(kinds, dtype=jnp.int32)
    slot_ids = jnp.arange(tile, dtype=jnp.int32)
    incoming = jnp.zeros((atoms_dev, width), jnp.bfloat16)
    stored = jnp.zeros((batches, atoms_dev), jnp.float32)
    energies = jnp.zeros((batches,), jnp.float32)
    weights = None
    for step in range(total_steps):
        batch = step - position
        valid = jnp.logical_and(batch >= 0, batch < batches)
        keep = jnp.logical_and(valid, is_last)
        index = jnp.clip(batch, 0, batches - 1)
        species = lax.dynamic_index_in_dim(tile_species, index, 0, keepdims=False)
        fill = lax.dynamic_index_in_dim(tile_fill, index, 0, keepdims=False)
        first = descriptors[min(step, batches - 1)]
        source = jnp.where(position == 0, first, incoming).reshape(tiles_dev, tile, width)
        if step == 0:
            weights = lax.all_gather(layer_weight[0], "dp", axis=1, tiled=True)
            product = grouped_product(source, weights, species)
        else:
            product = grouped_product(source, weights, species)
        onehot = (species[:, None] == kind_ids[None, :]).astype(jnp.float32)
        active = smooth_unit(product + table_rows(onehot, bias)[:, None, :])
        readout_rows = table_rows(onehot, readout)
        offsets = table_rows(onehot, self_energy[:, None])
        values = jnp.sum(active * readout_rows[:, None, :], axis=-1) + offsets
        present = slot_ids[None, :] < fill[:, None]
        values = jnp.where(jnp.logical_and(present, keep), values, jnp.float32(0.0)).reshape(
            atoms_dev
        )
        stored = stored.at[index].add(values)
        term = jnp.sum(values) / atoms_all
        finished = step - (sections - 1)
        if 0 <= finished < batches:
            energies = energies.at[finished].set(lax.psum(term, ("section", "dp")))
        if step < total_steps - 1:
            incoming = shifted(active.astype(jnp.bfloat16).reshape(atoms_dev, width), "section", 1)
    received = lax.all_to_all(stored, "section", split_axis=0, concat_axis=0, tiled=True)
    mine = received[sections - 1]
    return (mine[None, :], energies)


def solution(mesh):
    placed = (
        P(None, "dp", None),
        P("section", None, "dp", None),
        P("section", None, None),
        P(),
        P(),
        P(None, "dp"),
        P(None, "dp"),
    )
    return jax.shard_map(
        shards, mesh=mesh, in_specs=placed, out_specs=(P("section", "dp"), P()), check_vma=False
    )
```

profile of v0, /device:TPU:12, one launch (start us, length us, event | category | flops | bytes accessed | tf_op | source)
XLA Modules:
  0.0 464.9 jit_solution(16702947367663745943)
XLA Ops:
  12.9 146.2 %all-gather.3.cloned.1.call-done = bf16[1,8,1024,1024]{3,2,1,0:T(8,128)(2,1)} async-done(((bf16[1,8,128,1024]{3,2,1,0:T(8,128)(2,1)}), bf16[1,8,1024,1024]{3,2,1,0:T(8,128)(2,1)}) %all-gather.3.cloned.1.call-update) | async-done | bytes 16777232 | tf_op jit(solution)/shard_map/all_gather | solution.py:53
  159.1 11.7 %fusion.131 = (bf16[8,512,1024]{2,1,0:T(8,128)(2,1)}, bf16[8,512,1024]{2,1,0:T(8,128)(2,1)}) fusion(bf16[8,1024,1024]{2,1,0:T(8,128)(2,1)} %bitcast.146), kind=kLoop, calls=%fused_computation.259 | loop fusion | bytes 33554432 | tf_op jit(solution)/shard_map/jit(_take)/gather | solution.py:18
  170.8 6.2 %gather_fusion = bf16[4,512,1024]{2,1,0:T(8,128)(2,1)} fusion(bf16[8,512,1024]{2,1,0:T(8,128)(2,1)} %get-tuple-element.168, s32[1024]{0:T(1024)S(1)} %pad_clamp_fusion.6), kind=kCustom, calls=%fused_computation.clone | custom fusion | bytes 8388624 | tf_op jit(solution)/shard_map/jit(_take)/gather | solution.py:18
  176.9 6.1 %gather_fusion.1 = bf16[4,512,1024]{2,1,0:T(8,128)(2,1)} fusion(bf16[8,512,1024]{2,1,0:T(8,128)(2,1)} %get-tuple-element.169, s32[1024]{0:T(1024)S(1)} %pad_clamp_fusion.6), kind=kCustom, calls=%fused_computation.1.clone | custom fusion | bytes 8388624 | tf_op jit(solution)/shard_map/jit(_take)/gather | solution.py:18
  183.1 5.4 %fusion.137 = (bf16[4,128,1024]{2,1,0:T(8,128)(2,1)S(1)}, f32[4,128]{1,0:T(4,128)S(1)}) fusion(f32[4,1024]{1,0:T(4,128)S(1)} %fusion.56, f32[4,1024]{1,0:T(4,128)S(1)} %fusion.47, bf16[4,128,1024]{2,1,0:T(8,128)(2,1)S(1)} %bitcast.147, bf16[4,512,1024]{2,1,0:T(8,128)(2,1)} %gather_fusion.1, bf16[4,512,1024]{2,1,0:T(8,128)(2,1)} %gather_fusion, ...), kind=kOutput, calls=%fused_computation.265 | convolution fusion | flops 1098907136 | bytes 10520580 | tf_op jit(solution)/shard_map/tai,tio->tao/dot_general | solution.py:19
  188.5 3.4 collective-permute-start
  193.5 6.2 %gather_fusion.2 = bf16[4,512,1024]{2,1,0:T(8,128)(2,1)} fusion(bf16[8,512,1024]{2,1,0:T(8,128)(2,1)} %get-tuple-element.168, s32[1024]{0:T(1024)S(1)} %pad_clamp_fusion.5), kind=kCustom, calls=%fused_computation.2.clone | custom fusion | bytes 8388624 | tf_op jit(solution)/shard_map/jit(_take)/gather | solution.py:18
  199.7 6.1 %gather_fusion.3 = bf16[4,512,1024]{2,1,0:T(8,128)(2,1)} fusion(bf16[8,512,1024]{2,1,0:T(8,128)(2,1)} %get-tuple-element.169, s32[1024]{0:T(1024)S(1)} %pad_clamp_fusion.5), kind=kCustom, calls=%fused_computation.3.clone | custom fusion | bytes 8388624 | tf_op jit(solution)/shard_map/jit(_take)/gather | solution.py:18
  205.8 10.8 %collective-permute-done = bf16[512,1024]{1,0:T(8,128)(2,1)S(1)} collective-permute-done((bf16[512,1024]{1,0:T(8,128)(2,1)S(1)}, bf16[512,1024]{1,0:T(8,128)(2,1)S(1)}, u32[]{:S(2)}, u32[]{:S(2)}) %collective-permute-start) | collective-permute-done | bytes 1048608 | tf_op jit(solution)/shard_map/ppermute | solution.py:10
  217.9 5.4 %fusion.136 = (bf16[4,128,1024]{2,1,0:T(8,128)(2,1)S(1)}, f32[4,128]{1,0:T(4,128)S(1)}) fusion(f32[4,1024]{1,0:T(4,128)S(1)} %fusion.55, f32[4,1024]{1,0:T(4,128)S(1)} %fusion.45, bf16[4,128,1024]{2,1,0:T(8,128)(2,1)S(1)} %bitcast.148, bf16[4,512,1024]{2,1,0:T(8,128)(2,1)} %gather_fusion.3, bf16[4,512,1024]{2,1,0:T(8,128)(2,1)} %gather_fusion.2, ...), kind=kOutput, calls=%fused_computation.264 | convolution fusion | flops 1098907136 | bytes 10520580 | tf_op jit(solution)/shard_map/tai,tio->tao/dot_general | solution.py:19
  223.3 2.5 collective-permute-start.1
  227.0 6.2 %gather_fusion.4 = bf16[4,512,1024]{2,1,0:T(8,128)(2,1)} fusion(bf16[8,512,1024]{2,1,0:T(8,128)(2,1)} %get-tuple-element.168, s32[1024]{0:T(1024)S(1)} %pad_clamp_fusion.4), kind=kCustom, calls=%fused_computation.4.clone | custom fusion | bytes 8388624 | tf_op jit(solution)/shard_map/jit(_take)/gather | solution.py:18
  233.2 6.1 %gather_fusion.5 = bf16[4,512,1024]{2,1,0:T(8,128)(2,1)} fusion(bf16[8,512,1024]{2,1,0:T(8,128)(2,1)} %get-tuple-element.169, s32[1024]{0:T(1024)S(1)} %pad_clamp_fusion.4), kind=kCustom, calls=%fused_computation.5.clone | custom fusion | bytes 8388624 | tf_op jit(solution)/shard_map/jit(_take)/gather | solution.py:18
  239.4 11.2 %collective-permute-done.1 = bf16[512,1024]{1,0:T(8,128)(2,1)S(1)} collective-permute-done((bf16[512,1024]{1,0:T(8,128)(2,1)S(1)}, bf16[512,1024]{1,0:T(8,128)(2,1)S(1)}, u32[]{:S(2)}, u32[]{:S(2)}) %collective-permute-start.1) | collective-permute-done | bytes 1048608 | tf_op jit(solution)/shard_map/ppermute | solution.py:10
  251.9 5.4 %fusion.135 = (bf16[4,128,1024]{2,1,0:T(8,128)(2,1)S(1)}, f32[4,128]{1,0:T(4,128)S(1)}) fusion(f32[4,1024]{1,0:T(4,128)S(1)} %fusion.54, f32[4,1024]{1,0:T(4,128)S(1)} %fusion.43, bf16[4,128,1024]{2,1,0:T(8,128)(2,1)S(1)} %bitcast.149, bf16[4,512,1024]{2,1,0:T(8,128)(2,1)} %gather_fusion.5, bf16[4,512,1024]{2,1,0:T(8,128)(2,1)} %gather_fusion.4, ...), kind=kOutput, calls=%fused_computation.263 | convolution fusion | flops 1098907136 | bytes 10520580 | tf_op jit(solution)/shard_map/tai,tio->tao/dot_general | solution.py:19
  260.3 6.2 %gather_fusion.6 = bf16[4,512,1024]{2,1,0:T(8,128)(2,1)} fusion(bf16[8,512,1024]{2,1,0:T(8,128)(2,1)} %get-tuple-element.168, s32[1024]{0:T(1024)S(1)} %pad_clamp_fusion.3), kind=kCustom, calls=%fused_computation.6.clone | custom fusion | bytes 8388624 | tf_op jit(solution)/shard_map/jit(_take)/gather | solution.py:18
  266.5 6.1 %gather_fusion.7 = bf16[4,512,1024]{2,1,0:T(8,128)(2,1)} fusion(bf16[8,512,1024]{2,1,0:T(8,128)(2,1)} %get-tuple-element.169, s32[1024]{0:T(1024)S(1)} %pad_clamp_fusion.3), kind=kCustom, calls=%fused_computation.7.clone | custom fusion | bytes 8388624 | tf_op jit(solution)/shard_map/jit(_take)/gather | solution.py:18
  272.6 11.2 %collective-permute-done.2 = bf16[512,1024]{1,0:T(8,128)(2,1)S(1)} collective-permute-done((bf16[512,1024]{1,0:T(8,128)(2,1)S(1)}, bf16[512,1024]{1,0:T(8,128)(2,1)S(1)}, u32[]{:S(2)}, u32[]{:S(2)}) %collective-permute-start.2) | collective-permute-done | bytes 1048608 | tf_op jit(solution)/shard_map/ppermute | solution.py:10
  285.1 5.4 %fusion.134 = (bf16[4,128,1024]{2,1,0:T(8,128)(2,1)S(1)}, f32[4,128]{1,0:T(4,128)S(1)}) fusion(f32[4,1024]{1,0:T(4,128)S(1)} %fusion.53, f32[4,1024]{1,0:T(4,128)S(1)} %fusion.41, bf16[4,128,1024]{2,1,0:T(8,128)(2,1)S(1)} %bitcast.150, bf16[4,512,1024]{2,1,0:T(8,128)(2,1)} %gather_fusion.7, bf16[4,512,1024]{2,1,0:T(8,128)(2,1)} %gather_fusion.6, ...), kind=kOutput, calls=%fused_computation.262 | convolution fusion | flops 1098907136 | bytes 10520580 | tf_op jit(solution)/shard_map/tai,tio->tao/dot_general | solution.py:19
  293.5 6.3 %gather_fusion.8 = bf16[4,512,1024]{2,1,0:T(8,128)(2,1)} fusion(bf16[8,512,1024]{2,1,0:T(8,128)(2,1)} %get-tuple-element.168, s32[1024]{0:T(1024)S(1)} %pad_clamp_fusion.2), kind=kCustom, calls=%fused_computation.8.clone | custom fusion | bytes 8388624 | tf_op jit(solution)/shard_map/jit(_take)/gather | solution.py:18
  299.8 6.1 %gather_fusion.9 = bf16[4,512,1024]{2,1,0:T(8,128)(2,1)} fusion(bf16[8,512,1024]{2,1,0:T(8,128)(2,1)} %get-tuple-element.169, s32[1024]{0:T(1024)S(1)} %pad_clamp_fusion.2), kind=kCustom, calls=%fused_computation.9.clone | custom fusion | bytes 8388624 | tf_op jit(solution)/shard_map/jit(_take)/gather | solution.py:18
  305.9 6.2 %gather_fusion.10 = bf16[4,512,1024]{2,1,0:T(8,128)(2,1)} fusion(bf16[8,512,1024]{2,1,0:T(8,128)(2,1)} %get-tuple-element.168, s32[1024]{0:T(1024)S(1)} %pad_clamp_fusion.1), kind=kCustom, calls=%fused_computation.10.clone | custom fusion | bytes 8388624 | tf_op jit(solution)/shard_map/jit(_take)/gather | solution.py:18
  312.1 6.2 %gather_fusion.11 = bf16[4,512,1024]{2,1,0:T(8,128)(2,1)} fusion(bf16[8,512,1024]{2,1,0:T(8,128)(2,1)} %get-tuple-element.169, s32[1024]{0:T(1024)S(1)} %pad_clamp_fusion.1), kind=kCustom, calls=%fused_computation.11.clone | custom fusion | bytes 8388624 | tf_op jit(solution)/shard_map/jit(_take)/gather | solution.py:18
  318.2 6.1 %gather_fusion.12 = bf16[4,512,1024]{2,1,0:T(8,128)(2,1)} fusion(bf16[8,512,1024]{2,1,0:T(8,128)(2,1)} %get-tuple-element.168, s32[1024]{0:T(1024)S(1)} %pad_clamp_fusion), kind=kCustom, calls=%fused_computation.12.clone | custom fusion | bytes 8388624 | tf_op jit(solution)/shard_map/jit(_take)/gather | solution.py:18
  324.4 6.2 %gather_fusion.13 = bf16[4,512,1024]{2,1,0:T(8,128)(2,1)} fusion(bf16[8,512,1024]{2,1,0:T(8,128)(2,1)} %get-tuple-element.169, s32[1024]{0:T(1024)S(1)} %pad_clamp_fusion), kind=kCustom, calls=%fused_computation.13.clone | custom fusion | bytes 8388624 | tf_op jit(solution)/shard_map/jit(_take)/gather | solution.py:18
  332.6 5.4 %fusion.133 = (bf16[4,128,1024]{2,1,0:T(8,128)(2,1)S(1)}, f32[4,128]{1,0:T(4,128)S(1)}) fusion(f32[4,1024]{1,0:T(4,128)S(1)} %fusion.52, f32[4,1024]{1,0:T(4,128)S(1)} %fusion.39, bf16[4,128,1024]{2,1,0:T(8,128)(2,1)S(1)} %bitcast.151, bf16[4,512,1024]{2,1,0:T(8,128)(2,1)} %gather_fusion.9, bf16[4,512,1024]{2,1,0:T(8,128)(2,1)} %gather_fusion.8, ...), kind=kOutput, calls=%fused_computation.261 | convolution fusion | flops 1098907136 | bytes 10520580 | tf_op jit(solution)/shard_map/tai,tio->tao/dot_general | solution.py:19
  342.2 21.4 %collective-permute-done.4 = bf16[512,1024]{1,0:T(8,128)(2,1)S(1)} collective-permute-done((bf16[512,1024]{1,0:T(8,128)(2,1)S(1)}, bf16[512,1024]{1,0:T(8,128)(2,1)S(1)}, u32[]{:S(2)}, u32[]{:S(2)}) %collective-permute-start.4) | collective-permute-done | bytes 1048608 | tf_op jit(solution)/shard_map/ppermute | solution.py:10
  364.9 5.4 %fusion.132 = (bf16[4,128,1024]{2,1,0:T(8,128)(2,1)S(1)}, f32[4,128]{1,0:T(4,128)S(1)}) fusion(f32[4,1024]{1,0:T(4,128)S(1)} %fusion.51, f32[4,1024]{1,0:T(4,128)S(1)} %fusion.37, bf16[4,128,1024]{2,1,0:T(8,128)(2,1)S(1)} %bitcast.152, bf16[4,512,1024]{2,1,0:T(8,128)(2,1)} %gather_fusion.11, bf16[4,512,1024]{2,1,0:T(8,128)(2,1)} %gather_fusion.10, ...), kind=kOutput, calls=%fused_computation.260 | convolution fusion | flops 1098907136 | bytes 10520580 | tf_op jit(solution)/shard_map/tai,tio->tao/dot_general | solution.py:19
  376.3 18.7 %collective-permute-done.5 = bf16[512,1024]{1,0:T(8,128)(2,1)S(1)} collective-permute-done((bf16[512,1024]{1,0:T(8,128)(2,1)S(1)}, bf16[512,1024]{1,0:T(8,128)(2,1)S(1)}, u32[]{:S(2)}, u32[]{:S(2)}) %collective-permute-start.5) | collective-permute-done | bytes 1048608 | tf_op jit(solution)/shard_map/ppermute | solution.py:10
  396.4 5.4 %multiply_reduce_fusion = f32[4,128]{1,0:T(4,128)S(1)} fusion(bf16[4,128,1024]{2,1,0:T(8,128)(2,1)S(1)} %bitcast.153, bf16[4,512,1024]{2,1,0:T(8,128)(2,1)} %gather_fusion.13, bf16[4,512,1024]{2,1,0:T(8,128)(2,1)} %gather_fusion.12, pred[4]{0:T(512)(128)(4,1)S(1)} %get-tuple-element.154, f32[4,1024]{1,0:T(4,128)S(1)} %fusion.50, f32[4,1024]{1,0:T(4,128)S(1)} %fusion.35), kind=kOutput, calls=%fused_computation.56 | convolution fusion | flops 1098382848 | bytes 9472004 | tf_op jit(solution)/shard_map/tai,tio->tao/dot_general | solution.py:19
  403.7 3.3 all-to-all-start
  409.5 45.5 %all-reduce.1 = (f32[1]{0:T(128)}, f32[1]{0:T(128)}, f32[1]{0:T(128)}, f32[1]{0:T(128)}) all-reduce(f32[1]{0:T(128)} %bitcast.62, f32[1]{0:T(128)} %bitcast.63, f32[1]{0:T(128)} %bitcast.64, f32[1]{0:T(128)} %bitcast.65), channel_id=1, replica_groups=mesh['section'=4,'dp'=8] {'section','dp'}, use_global_device_ids=true, to_apply=%region_15.17 | all-reduce | flops 4 | bytes 32 | tf_op jit(solution)/shard_map/psum | solution.py:70
  (89 shorter events, 38.0 us)
Async XLA Ops:
  7.2 3.3 copy-start
  7.2 151.9 %all-gather.3.cloned.1.call-start = ((), (), s32[]{:S(2)}) async-start(), calls=%async_computation.1 | async-start | bytes 18874368 | tf_op jit(solution)/shard_map/all_gather | solution.py:53
  183.1 8.8 %copy-start.2 = (s32[2]{0:T(128)S(1)}, s32[2]{0:T(128)}, u32[]{:S(2)}) copy-start(s32[2]{0:T(128)} %constant.301.clone.1) | copy-start | bytes 28
  183.1 9.6 %copy-start.4 = (f32[8]{0:T(128)S(1)}, f32[8]{0:T(128)}, u32[]{:S(2)}) copy-start(f32[8]{0:T(128)} %param.35) | copy-start | bytes 100
  183.1 10.2 %copy-start.3 = (f32[8,1024]{1,0:T(8,128)S(1)}, f32[8,1024]{1,0:T(8,128)}, u32[]{:S(2)}) copy-start(f32[8,1024]{1,0:T(8,128)} %param.34) | copy-start | bytes 98308
  188.5 28.1 %collective-permute-start = (bf16[512,1024]{1,0:T(8,128)(2,1)S(1)}, bf16[512,1024]{1,0:T(8,128)(2,1)S(1)}, u32[]{:S(2)}, u32[]{:S(2)}) collective-permute-start(bf16[512,1024]{1,0:T(8,128)(2,1)S(1)} %bitcast.164), channel_id=1, source_target_pairs={{0,8},{8,16},{16,24},{1,9},{9,17},{17,25},{2,10},{10,18},{18,26},{... | collective-permute-start | bytes 3145736 | tf_op jit(solution)/shard_map/ppermute | solution.py:10
  223.3 27.3 %collective-permute-start.1 = (bf16[512,1024]{1,0:T(8,128)(2,1)S(1)}, bf16[512,1024]{1,0:T(8,128)(2,1)S(1)}, u32[]{:S(2)}, u32[]{:S(2)}) collective-permute-start(bf16[512,1024]{1,0:T(8,128)(2,1)S(1)} %bitcast.166), channel_id=1, source_target_pairs={{0,8},{8,16},{16,24},{1,9},{9,17},{17,25},{2,10},{10,18},{18,26},{... | collective-permute-start | bytes 3145736 | tf_op jit(solution)/shard_map/ppermute | solution.py:10
  257.4 26.4 %collective-permute-start.2 = (bf16[512,1024]{1,0:T(8,128)(2,1)S(1)}, bf16[512,1024]{1,0:T(8,128)(2,1)S(1)}, u32[]{:S(2)}, u32[]{:S(2)}) collective-permute-start(bf16[512,1024]{1,0:T(8,128)(2,1)S(1)} %bitcast.165), channel_id=1, source_target_pairs={{0,8},{8,16},{16,24},{1,9},{9,17},{17,25},{2,10},{10,18},{18,26},{... | collective-permute-start | bytes 3145736 | tf_op jit(solution)/shard_map/ppermute | solution.py:10
  285.1 7.5 %copy-start.1 = (s32[4,4]{1,0:T(4,128)S(1)}, s32[4,4]{1,0:T(4,128)}, u32[]{:S(2)}) copy-start(s32[4,4]{1,0:T(4,128)} %param.37) | copy-start | bytes 196
  290.5 40.7 %collective-permute-start.3 = (bf16[512,1024]{1,0:T(8,128)(2,1)S(1)}, bf16[512,1024]{1,0:T(8,128)(2,1)S(1)}, u32[]{:S(2)}, u32[]{:S(2)}) collective-permute-start(bf16[512,1024]{1,0:T(8,128)(2,1)S(1)} %bitcast.161), channel_id=1, source_target_pairs={{0,8},{8,16},{16,24},{1,9},{9,17},{17,25},{2,10},{10,18},{18,26},{... | collective-permute-start | bytes 3145736 | tf_op jit(solution)/shard_map/ppermute | solution.py:10
  338.0 25.6 %collective-permute-start.4 = (bf16[512,1024]{1,0:T(8,128)(2,1)S(1)}, bf16[512,1024]{1,0:T(8,128)(2,1)S(1)}, u32[]{:S(2)}, u32[]{:S(2)}) collective-permute-start(bf16[512,1024]{1,0:T(8,128)(2,1)S(1)} %bitcast.163), channel_id=1, source_target_pairs={{0,8},{8,16},{16,24},{1,9},{9,17},{17,25},{2,10},{10,18},{18,26},{... | collective-permute-start | bytes 3145736 | tf_op jit(solution)/shard_map/ppermute | solution.py:10
  370.4 24.7 %collective-permute-start.5 = (bf16[512,1024]{1,0:T(8,128)(2,1)S(1)}, bf16[512,1024]{1,0:T(8,128)(2,1)S(1)}, u32[]{:S(2)}, u32[]{:S(2)}) collective-permute-start(bf16[512,1024]{1,0:T(8,128)(2,1)S(1)} %bitcast.162), channel_id=1, source_target_pairs={{0,8},{8,16},{16,24},{1,9},{9,17},{17,25},{2,10},{10,18},{18,26},{... | collective-permute-start | bytes 3145736 | tf_op jit(solution)/shard_map/ppermute | solution.py:10
  403.7 53.8 %all-to-all-start = ((f32[4,1,512]{2,1,0:T(1,128)}), f32[4,1,512]{2,1,0:T(1,128)S(1)}, u32[]{:S(2)}, u32[]{:S(2)}) async-start(f32[4,1,512]{2,1,0:T(1,128)} %constant_dynamic-update-slice_fusion), calls=%async_computation | async-start | bytes 16384 | tf_op jit(solution)/shard_map/all_to_all | solution.py:73
  457.4 0.6 copy-start.5
Sparse Core Ops, SparseCore 0:
  9.6 149.4 all-gather.2
where the time goes:
time: 466 us; the launch traced here: 465 us
  waiting for transfers between devices  220 us (47%)
  local copies, waits for them, and re-layouts  102 us (22%)
  blocking collectives  45.5 us (10%)
  matrix products  42.8 us (9%)
  other arithmetic  20.5 us (4%)
  starting transfers between devices  17.1 us (4%)
  between operations  17 us (4%)
    all_gather x1, waiting for transfers between devices, shards(): weights = lax.all_gather(layer_weight[0], 'dp', axis=1, tiled=True)  146 us
    gather x15, local copies, waits for them, and re-layouts, grouped_product(): chosen = jnp.take(weights, species, axis=0)  97.9 us
    ppermute x6, waiting for transfers between devices, shifted(): return lax.ppermute(block, axis, route)  73.3 us
    psum x1, blocking collectives, shards(): energies = energies.at[finished].set(lax.psum(term, ('section', 'dp')))  45.5 us
    dot_general x7, matrix products, grouped_product(): jnp.einsum('tai,tio->tao', source, chosen, preferred_element_type=jnp.flo...  37.9 us
    ppermute x6, starting transfers between devices, shifted(): return lax.ppermute(block, axis, route)  13.7 us
  transfers between devices with their start and end apart: 8, of which 6 were waited for; matrix products, arithmetic and copies ran while one was open for 20% of the time, Pallas kernels for 0%

commit v1 on v0

--- a/solution.py
+++ b/solution.py
@@ -50,7 +50,9 @@
         first = descriptors[min(step, batches - 1)]
         source = jnp.where(position == 0, first, incoming).reshape(tiles_dev, tile, width)
         if step == 0:
-            weights = lax.all_gather(layer_weight[0], "dp", axis=1, tiled=True)
+            own = layer_weight[0]
+            parts = lax.all_gather(own, "dp", axis=0, tiled=False)
+            weights = jnp.concatenate(parts, axis=1)
             product = grouped_product(source, weights, species)
         else:
             product = grouped_product(source, weights, species)

time: 466 us -> 466 us (level)
  no operation moved by 1% of the time
where the time goes in v1:
time: 466 us; the launch traced here: 465 us
  waiting for transfers between devices  220 us (47%)
  local copies, waits for them, and re-layouts  102 us (22%)
  blocking collectives  45.5 us (10%)
  matrix products  42.8 us (9%)
  other arithmetic  20.5 us (4%)
  starting transfers between devices  17.1 us (4%)
  between operations  17 us (4%)
    all_gather x1, waiting for transfers between devices, shards(): parts = lax.all_gather(own, 'dp', axis=0, tiled=False)  146 us
    gather x15, local copies, waits for them, and re-layouts, grouped_product(): chosen = jnp.take(weights, species, axis=0)  97.9 us
    ppermute x6, waiting for transfers between devices, shifted(): return lax.ppermute(block, axis, route)  73.3 us
    psum x1, blocking collectives, shards(): energies = energies.at[finished].set(lax.psum(term, ('section', 'dp')))  45.5 us
    dot_general x7, matrix products, grouped_product(): jnp.einsum('tai,tio->tao', source, chosen, preferred_element_type=jnp.flo...  37.9 us
    ppermute x6, starting transfers between devices, shifted(): return lax.ppermute(block, axis, route)  13.7 us
  transfers between devices with their start and end apart: 8, of which 6 were waited for; matrix products, arithmetic and copies ran while one was open for 20% of the time, Pallas kernels for 0%

profile of v1, /device:TPU:12, one launch (start us, length us, event | category | flops | bytes accessed | tf_op | source)
XLA Modules:
  0.0 464.9 jit_solution(16702947367663745943)
XLA Ops:
  12.9 146.2 %all-gather.2.cloned.1.call-done = bf16[8,8,128,1024]{3,2,0,1:T(8,128)(2,1)} async-done(((bf16[1,8,128,1024]{3,2,0,1:T(8,128)(2,1)}), bf16[8,8,128,1024]{3,2,0,1:T(8,128)(2,1)}) %all-gather.2.cloned.1.call-update) | async-done | bytes 16777232 | tf_op jit(solution)/shard_map/all_gather | solution.py:54
  159.1 11.7 %fusion.131 = (bf16[8,512,1024]{2,1,0:T(8,128)(2,1)}, bf16[8,512,1024]{2,1,0:T(8,128)(2,1)}) fusion(bf16[8,1024,1024]{2,1,0:T(8,128)(2,1)} %bitcast.149), kind=kLoop, calls=%fused_computation.259 | loop fusion | bytes 33554432 | tf_op jit(solution)/shard_map/jit(_take)/gather | solution.py:18
  170.8 6.2 %gather_fusion = bf16[4,512,1024]{2,1,0:T(8,128)(2,1)} fusion(bf16[8,512,1024]{2,1,0:T(8,128)(2,1)} %get-tuple-element.168, s32[1024]{0:T(1024)S(1)} %pad_clamp_fusion.6), kind=kCustom, calls=%fused_computation.clone | custom fusion | bytes 8388624 | tf_op jit(solution)/shard_map/jit(_take)/gather | solution.py:18
  176.9 6.1 %gather_fusion.1 = bf16[4,512,1024]{2,1,0:T(8,128)(2,1)} fusion(bf16[8,512,1024]{2,1,0:T(8,128)(2,1)} %get-tuple-element.169, s32[1024]{0:T(1024)S(1)} %pad_clamp_fusion.6), kind=kCustom, calls=%fused_computation.1.clone | custom fusion | bytes 8388624 | tf_op jit(solution)/shard_map/jit(_take)/gather | solution.py:18
  183.1 5.4 %fusion.137 = (bf16[4,128,1024]{2,1,0:T(8,128)(2,1)S(1)}, f32[4,128]{1,0:T(4,128)S(1)}) fusion(f32[4,1024]{1,0:T(4,128)S(1)} %fusion.56, f32[4,1024]{1,0:T(4,128)S(1)} %fusion.47, bf16[4,128,1024]{2,1,0:T(8,128)(2,1)S(1)} %bitcast.151, bf16[4,512,1024]{2,1,0:T(8,128)(2,1)} %gather_fusion.1, bf16[4,512,1024]{2,1,0:T(8,128)(2,1)} %gather_fusion, ...), kind=kOutput, calls=%fused_computation.265 | convolution fusion | flops 1098907136 | bytes 10520580 | tf_op jit(solution)/shard_map/tai,tio->tao/dot_general | solution.py:19
  188.5 3.4 collective-permute-start
  193.5 6.2 %gather_fusion.2 = bf16[4,512,1024]{2,1,0:T(8,128)(2,1)} fusion(bf16[8,512,1024]{2,1,0:T(8,128)(2,1)} %get-tuple-element.168, s32[1024]{0:T(1024)S(1)} %pad_clamp_fusion.5), kind=kCustom, calls=%fused_computation.2.clone | custom fusion | bytes 8388624 | tf_op jit(solution)/shard_map/jit(_take)/gather | solution.py:18
  199.7 6.1 %gather_fusion.3 = bf16[4,512,1024]{2,1,0:T(8,128)(2,1)} fusion(bf16[8,512,1024]{2,1,0:T(8,128)(2,1)} %get-tuple-element.169, s32[1024]{0:T(1024)S(1)} %pad_clamp_fusion.5), kind=kCustom, calls=%fused_computation.3.clone | custom fusion | bytes 8388624 | tf_op jit(solution)/shard_map/jit(_take)/gather | solution.py:18
  205.8 10.8 %collective-permute-done = bf16[512,1024]{1,0:T(8,128)(2,1)S(1)} collective-permute-done((bf16[512,1024]{1,0:T(8,128)(2,1)S(1)}, bf16[512,1024]{1,0:T(8,128)(2,1)S(1)}, u32[]{:S(2)}, u32[]{:S(2)}) %collective-permute-start) | collective-permute-done | bytes 1048608 | tf_op jit(solution)/shard_map/ppermute | solution.py:10
  217.9 5.4 %fusion.136 = (bf16[4,128,1024]{2,1,0:T(8,128)(2,1)S(1)}, f32[4,128]{1,0:T(4,128)S(1)}) fusion(f32[4,1024]{1,0:T(4,128)S(1)} %fusion.55, f32[4,1024]{1,0:T(4,128)S(1)} %fusion.45, bf16[4,128,1024]{2,1,0:T(8,128)(2,1)S(1)} %bitcast.152, bf16[4,512,1024]{2,1,0:T(8,128)(2,1)} %gather_fusion.3, bf16[4,512,1024]{2,1,0:T(8,128)(2,1)} %gather_fusion.2, ...), kind=kOutput, calls=%fused_computation.264 | convolution fusion | flops 1098907136 | bytes 10520580 | tf_op jit(solution)/shard_map/tai,tio->tao/dot_general | solution.py:19
  223.3 2.5 collective-permute-start.1
  227.0 6.2 %gather_fusion.4 = bf16[4,512,1024]{2,1,0:T(8,128)(2,1)} fusion(bf16[8,512,1024]{2,1,0:T(8,128)(2,1)} %get-tuple-element.168, s32[1024]{0:T(1024)S(1)} %pad_clamp_fusion.4), kind=kCustom, calls=%fused_computation.4.clone | custom fusion | bytes 8388624 | tf_op jit(solution)/shard_map/jit(_take)/gather | solution.py:18
  233.2 6.1 %gather_fusion.5 = bf16[4,512,1024]{2,1,0:T(8,128)(2,1)} fusion(bf16[8,512,1024]{2,1,0:T(8,128)(2,1)} %get-tuple-element.169, s32[1024]{0:T(1024)S(1)} %pad_clamp_fusion.4), kind=kCustom, calls=%fused_computation.5.clone | custom fusion | bytes 8388624 | tf_op jit(solution)/shard_map/jit(_take)/gather | solution.py:18
  239.4 11.2 %collective-permute-done.1 = bf16[512,1024]{1,0:T(8,128)(2,1)S(1)} collective-permute-done((bf16[512,1024]{1,0:T(8,128)(2,1)S(1)}, bf16[512,1024]{1,0:T(8,128)(2,1)S(1)}, u32[]{:S(2)}, u32[]{:S(2)}) %collective-permute-start.1) | collective-permute-done | bytes 1048608 | tf_op jit(solution)/shard_map/ppermute | solution.py:10
  251.9 5.4 %fusion.135 = (bf16[4,128,1024]{2,1,0:T(8,128)(2,1)S(1)}, f32[4,128]{1,0:T(4,128)S(1)}) fusion(f32[4,1024]{1,0:T(4,128)S(1)} %fusion.54, f32[4,1024]{1,0:T(4,128)S(1)} %fusion.43, bf16[4,128,1024]{2,1,0:T(8,128)(2,1)S(1)} %bitcast.153, bf16[4,512,1024]{2,1,0:T(8,128)(2,1)} %gather_fusion.5, bf16[4,512,1024]{2,1,0:T(8,128)(2,1)} %gather_fusion.4, ...), kind=kOutput, calls=%fused_computation.263 | convolution fusion | flops 1098907136 | bytes 10520580 | tf_op jit(solution)/shard_map/tai,tio->tao/dot_general | solution.py:19
  260.3 6.2 %gather_fusion.6 = bf16[4,512,1024]{2,1,0:T(8,128)(2,1)} fusion(bf16[8,512,1024]{2,1,0:T(8,128)(2,1)} %get-tuple-element.168, s32[1024]{0:T(1024)S(1)} %pad_clamp_fusion.3), kind=kCustom, calls=%fused_computation.6.clone | custom fusion | bytes 8388624 | tf_op jit(solution)/shard_map/jit(_take)/gather | solution.py:18
  266.5 6.1 %gather_fusion.7 = bf16[4,512,1024]{2,1,0:T(8,128)(2,1)} fusion(bf16[8,512,1024]{2,1,0:T(8,128)(2,1)} %get-tuple-element.169, s32[1024]{0:T(1024)S(1)} %pad_clamp_fusion.3), kind=kCustom, calls=%fused_computation.7.clone | custom fusion | bytes 8388624 | tf_op jit(solution)/shard_map/jit(_take)/gather | solution.py:18
  272.6 11.2 %collective-permute-done.2 = bf16[512,1024]{1,0:T(8,128)(2,1)S(1)} collective-permute-done((bf16[512,1024]{1,0:T(8,128)(2,1)S(1)}, bf16[512,1024]{1,0:T(8,128)(2,1)S(1)}, u32[]{:S(2)}, u32[]{:S(2)}) %collective-permute-start.2) | collective-permute-done | bytes 1048608 | tf_op jit(solution)/shard_map/ppermute | solution.py:10
  285.1 5.4 %fusion.134 = (bf16[4,128,1024]{2,1,0:T(8,128)(2,1)S(1)}, f32[4,128]{1,0:T(4,128)S(1)}) fusion(f32[4,1024]{1,0:T(4,128)S(1)} %fusion.53, f32[4,1024]{1,0:T(4,128)S(1)} %fusion.41, bf16[4,128,1024]{2,1,0:T(8,128)(2,1)S(1)} %bitcast.154, bf16[4,512,1024]{2,1,0:T(8,128)(2,1)} %gather_fusion.7, bf16[4,512,1024]{2,1,0:T(8,128)(2,1)} %gather_fusion.6, ...), kind=kOutput, calls=%fused_computation.262 | convolution fusion | flops 1098907136 | bytes 10520580 | tf_op jit(solution)/shard_map/tai,tio->tao/dot_general | solution.py:19
  293.5 6.3 %gather_fusion.8 = bf16[4,512,1024]{2,1,0:T(8,128)(2,1)} fusion(bf16[8,512,1024]{2,1,0:T(8,128)(2,1)} %get-tuple-element.168, s32[1024]{0:T(1024)S(1)} %pad_clamp_fusion.2), kind=kCustom, calls=%fused_computation.8.clone | custom fusion | bytes 8388624 | tf_op jit(solution)/shard_map/jit(_take)/gather | solution.py:18
  299.8 6.1 %gather_fusion.9 = bf16[4,512,1024]{2,1,0:T(8,128)(2,1)} fusion(bf16[8,512,1024]{2,1,0:T(8,128)(2,1)} %get-tuple-element.169, s32[1024]{0:T(1024)S(1)} %pad_clamp_fusion.2), kind=kCustom, calls=%fused_computation.9.clone | custom fusion | bytes 8388624 | tf_op jit(solution)/shard_map/jit(_take)/gather | solution.py:18
  305.9 6.2 %gather_fusion.10 = bf16[4,512,1024]{2,1,0:T(8,128)(2,1)} fusion(bf16[8,512,1024]{2,1,0:T(8,128)(2,1)} %get-tuple-element.168, s32[1024]{0:T(1024)S(1)} %pad_clamp_fusion.1), kind=kCustom, calls=%fused_computation.10.clone | custom fusion | bytes 8388624 | tf_op jit(solution)/shard_map/jit(_take)/gather | solution.py:18
  312.1 6.2 %gather_fusion.11 = bf16[4,512,1024]{2,1,0:T(8,128)(2,1)} fusion(bf16[8,512,1024]{2,1,0:T(8,128)(2,1)} %get-tuple-element.169, s32[1024]{0:T(1024)S(1)} %pad_clamp_fusion.1), kind=kCustom, calls=%fused_computation.11.clone | custom fusion | bytes 8388624 | tf_op jit(solution)/shard_map/jit(_take)/gather | solution.py:18
  318.2 6.1 %gather_fusion.12 = bf16[4,512,1024]{2,1,0:T(8,128)(2,1)} fusion(bf16[8,512,1024]{2,1,0:T(8,128)(2,1)} %get-tuple-element.168, s32[1024]{0:T(1024)S(1)} %pad_clamp_fusion), kind=kCustom, calls=%fused_computation.12.clone | custom fusion | bytes 8388624 | tf_op jit(solution)/shard_map/jit(_take)/gather | solution.py:18
  324.4 6.2 %gather_fusion.13 = bf16[4,512,1024]{2,1,0:T(8,128)(2,1)} fusion(bf16[8,512,1024]{2,1,0:T(8,128)(2,1)} %get-tuple-element.169, s32[1024]{0:T(1024)S(1)} %pad_clamp_fusion), kind=kCustom, calls=%fused_computation.13.clone | custom fusion | bytes 8388624 | tf_op jit(solution)/shard_map/jit(_take)/gather | solution.py:18
  332.6 5.4 %fusion.133 = (bf16[4,128,1024]{2,1,0:T(8,128)(2,1)S(1)}, f32[4,128]{1,0:T(4,128)S(1)}) fusion(f32[4,1024]{1,0:T(4,128)S(1)} %fusion.52, f32[4,1024]{1,0:T(4,128)S(1)} %fusion.39, bf16[4,128,1024]{2,1,0:T(8,128)(2,1)S(1)} %bitcast.155, bf16[4,512,1024]{2,1,0:T(8,128)(2,1)} %gather_fusion.9, bf16[4,512,1024]{2,1,0:T(8,128)(2,1)} %gather_fusion.8, ...), kind=kOutput, calls=%fused_computation.261 | convolution fusion | flops 1098907136 | bytes 10520580 | tf_op jit(solution)/shard_map/tai,tio->tao/dot_general | solution.py:19
  342.2 21.4 %collective-permute-done.4 = bf16[512,1024]{1,0:T(8,128)(2,1)S(1)} collective-permute-done((bf16[512,1024]{1,0:T(8,128)(2,1)S(1)}, bf16[512,1024]{1,0:T(8,128)(2,1)S(1)}, u32[]{:S(2)}, u32[]{:S(2)}) %collective-permute-start.4) | collective-permute-done | bytes 1048608 | tf_op jit(solution)/shard_map/ppermute | solution.py:10
  364.9 5.4 %fusion.132 = (bf16[4,128,1024]{2,1,0:T(8,128)(2,1)S(1)}, f32[4,128]{1,0:T(4,128)S(1)}) fusion(f32[4,1024]{1,0:T(4,128)S(1)} %fusion.51, f32[4,1024]{1,0:T(4,128)S(1)} %fusion.37, bf16[4,128,1024]{2,1,0:T(8,128)(2,1)S(1)} %bitcast.156, bf16[4,512,1024]{2,1,0:T(8,128)(2,1)} %gather_fusion.11, bf16[4,512,1024]{2,1,0:T(8,128)(2,1)} %gather_fusion.10, ...), kind=kOutput, calls=%fused_computation.260 | convolution fusion | flops 1098907136 | bytes 10520580 | tf_op jit(solution)/shard_map/tai,tio->tao/dot_general | solution.py:19
  376.3 18.7 %collective-permute-done.5 = bf16[512,1024]{1,0:T(8,128)(2,1)S(1)} collective-permute-done((bf16[512,1024]{1,0:T(8,128)(2,1)S(1)}, bf16[512,1024]{1,0:T(8,128)(2,1)S(1)}, u32[]{:S(2)}, u32[]{:S(2)}) %collective-permute-start.5) | collective-permute-done | bytes 1048608 | tf_op jit(solution)/shard_map/ppermute | solution.py:10
  396.4 5.4 %multiply_reduce_fusion = f32[4,128]{1,0:T(4,128)S(1)} fusion(bf16[4,128,1024]{2,1,0:T(8,128)(2,1)S(1)} %bitcast.157, bf16[4,512,1024]{2,1,0:T(8,128)(2,1)} %gather_fusion.13, bf16[4,512,1024]{2,1,0:T(8,128)(2,1)} %gather_fusion.12, pred[4]{0:T(512)(128)(4,1)S(1)} %get-tuple-element.154, f32[4,1024]{1,0:T(4,128)S(1)} %fusion.50, f32[4,1024]{1,0:T(4,128)S(1)} %fusion.35), kind=kOutput, calls=%fused_computation.56 | convolution fusion | flops 1098382848 | bytes 9472004 | tf_op jit(solution)/shard_map/tai,tio->tao/dot_general | solution.py:19
  403.7 3.3 all-to-all-start
  409.5 45.5 %all-reduce.1 = (f32[1]{0:T(128)}, f32[1]{0:T(128)}, f32[1]{0:T(128)}, f32[1]{0:T(128)}) all-reduce(f32[1]{0:T(128)} %bitcast.65, f32[1]{0:T(128)} %bitcast.66, f32[1]{0:T(128)} %bitcast.67, f32[1]{0:T(128)} %bitcast.68), channel_id=1, replica_groups=mesh['section'=4,'dp'=8] {'section','dp'}, use_global_device_ids=true, to_apply=%region_15.17 | all-reduce | flops 4 | bytes 32 | tf_op jit(solution)/shard_map/psum | solution.py:72
  (89 shorter events, 38.0 us)
Async XLA Ops:
  7.2 3.3 copy-start
  7.2 151.9 %all-gather.2.cloned.1.call-start = ((), (), s32[]{:S(2)}) async-start(), calls=%async_computation.1 | async-start | bytes 18874368 | tf_op jit(solution)/shard_map/all_gather | solution.py:54
  183.1 8.8 %copy-start.2 = (s32[2]{0:T(128)S(1)}, s32[2]{0:T(128)}, u32[]{:S(2)}) copy-start(s32[2]{0:T(128)} %constant.301.clone.1) | copy-start | bytes 28
  183.1 9.6 %copy-start.4 = (f32[8]{0:T(128)S(1)}, f32[8]{0:T(128)}, u32[]{:S(2)}) copy-start(f32[8]{0:T(128)} %param.35) | copy-start | bytes 100
  183.1 10.2 %copy-start.3 = (f32[8,1024]{1,0:T(8,128)S(1)}, f32[8,1024]{1,0:T(8,128)}, u32[]{:S(2)}) copy-start(f32[8,1024]{1,0:T(8,128)} %param.34) | copy-start | bytes 98308
  188.5 28.1 %collective-permute-start = (bf16[512,1024]{1,0:T(8,128)(2,1)S(1)}, bf16[512,1024]{1,0:T(8,128)(2,1)S(1)}, u32[]{:S(2)}, u32[]{:S(2)}) collective-permute-start(bf16[512,1024]{1,0:T(8,128)(2,1)S(1)} %bitcast.168), channel_id=1, source_target_pairs={{0,8},{8,16},{16,24},{1,9},{9,17},{17,25},{2,10},{10,18},{18,26},{... | collective-permute-start | bytes 3145736 | tf_op jit(solution)/shard_map/ppermute | solution.py:10
  223.3 27.3 %collective-permute-start.1 = (bf16[512,1024]{1,0:T(8,128)(2,1)S(1)}, bf16[512,1024]{1,0:T(8,128)(2,1)S(1)}, u32[]{:S(2)}, u32[]{:S(2)}) collective-permute-start(bf16[512,1024]{1,0:T(8,128)(2,1)S(1)} %bitcast.170), channel_id=1, source_target_pairs={{0,8},{8,16},{16,24},{1,9},{9,17},{17,25},{2,10},{10,18},{18,26},{... | collective-permute-start | bytes 3145736 | tf_op jit(solution)/shard_map/ppermute | solution.py:10
  257.4 26.4 %collective-permute-start.2 = (bf16[512,1024]{1,0:T(8,128)(2,1)S(1)}, bf16[512,1024]{1,0:T(8,128)(2,1)S(1)}, u32[]{:S(2)}, u32[]{:S(2)}) collective-permute-start(bf16[512,1024]{1,0:T(8,128)(2,1)S(1)} %bitcast.169), channel_id=1, source_target_pairs={{0,8},{8,16},{16,24},{1,9},{9,17},{17,25},{2,10},{10,18},{18,26},{... | collective-permute-start | bytes 3145736 | tf_op jit(solution)/shard_map/ppermute | solution.py:10
  285.1 7.5 %copy-start.1 = (s32[4,4]{1,0:T(4,128)S(1)}, s32[4,4]{1,0:T(4,128)}, u32[]{:S(2)}) copy-start(s32[4,4]{1,0:T(4,128)} %param.37) | copy-start | bytes 196
  290.5 40.7 %collective-permute-start.3 = (bf16[512,1024]{1,0:T(8,128)(2,1)S(1)}, bf16[512,1024]{1,0:T(8,128)(2,1)S(1)}, u32[]{:S(2)}, u32[]{:S(2)}) collective-permute-start(bf16[512,1024]{1,0:T(8,128)(2,1)S(1)} %bitcast.165), channel_id=1, source_target_pairs={{0,8},{8,16},{16,24},{1,9},{9,17},{17,25},{2,10},{10,18},{18,26},{... | collective-permute-start | bytes 3145736 | tf_op jit(solution)/shard_map/ppermute | solution.py:10
  338.0 25.6 %collective-permute-start.4 = (bf16[512,1024]{1,0:T(8,128)(2,1)S(1)}, bf16[512,1024]{1,0:T(8,128)(2,1)S(1)}, u32[]{:S(2)}, u32[]{:S(2)}) collective-permute-start(bf16[512,1024]{1,0:T(8,128)(2,1)S(1)} %bitcast.167), channel_id=1, source_target_pairs={{0,8},{8,16},{16,24},{1,9},{9,17},{17,25},{2,10},{10,18},{18,26},{... | collective-permute-start | bytes 3145736 | tf_op jit(solution)/shard_map/ppermute | solution.py:10
  370.4 24.7 %collective-permute-start.5 = (bf16[512,1024]{1,0:T(8,128)(2,1)S(1)}, bf16[512,1024]{1,0:T(8,128)(2,1)S(1)}, u32[]{:S(2)}, u32[]{:S(2)}) collective-permute-start(bf16[512,1024]{1,0:T(8,128)(2,1)S(1)} %bitcast.166), channel_id=1, source_target_pairs={{0,8},{8,16},{16,24},{1,9},{9,17},{17,25},{2,10},{10,18},{18,26},{... | collective-permute-start | bytes 3145736 | tf_op jit(solution)/shard_map/ppermute | solution.py:10
  403.7 53.8 %all-to-all-start = ((f32[4,1,512]{2,1,0:T(1,128)}), f32[4,1,512]{2,1,0:T(1,128)S(1)}, u32[]{:S(2)}, u32[]{:S(2)}) async-start(f32[4,1,512]{2,1,0:T(1,128)} %constant_dynamic-update-slice_fusion), calls=%async_computation | async-start | bytes 16384 | tf_op jit(solution)/shard_map/all_to_all | solution.py:75
  457.4 0.6 copy-start.5
Sparse Core Ops, SparseCore 0:
  9.6 149.4 all-gather.1
